TPU v7x, 32 devices: a whole 2x2x4 slice. The times are simulated.
32 devices in a mesh: shift: 8 (over y, x, core), dom: 4 (over z).
Axes of the slice: x: 2, y: 2, z: 4, core: 2. Of those that a mesh axis runs over, the one named last changes fastest.
Arguments:
- samples: float32 [32, 64, 1024], P('dom'), may hold values from -6 to 6
- potential: float32 [32, 1024], P('dom'), may hold values from 0 to 4
Outputs:
- subspace: float32 [32, 64, 1024], P('dom')
- reduced_h: float32 [64, 64], replicated
- reduced_b: float32 [64, 64], replicated
All inputs are finite; a program needn't handle non-finite values.
Results may differ from a plain program's by a relative error of at most 0.00027.
Values sent between devices are 32-bit elements; how exact they have to be, the bound alone decides.
No kernel may reach another device: no remote copies, remote signals or barrier semaphores. Data moves between devices by JAX's collectives and lax.ppermute only.
A program may use at most 128 MiB of HBM per device.

v0:
```python
import jax
import jax.numpy as jnp
from jax import lax
from jax.sharding import PartitionSpec as P

NX = 32
NY = 32
CENTRE = 3.0
RADIUS = 2.0
RIDGE = 0.01


def extended_2(x, sides, width):
    for axis, dim in sides:
        count, length = (lax.axis_size(axis), x.shape[dim])
        up = [(i, (i + 1) % count) for i in range(count - 1)]
        down = [(j, i) for i, j in up]
        last = lax.slice_in_dim(x, length - width, length, axis=dim)
        first = lax.slice_in_dim(x, 0, width, axis=dim)
        before = lax.ppermute(last, axis, up)
        after = lax.ppermute(first, axis, down)
        x = jnp.concatenate([before, x, after], axis=dim)
    return x


def plane_sum(values):
    extent = values.shape[-1]
    leading = [(0, 0)] * (values.ndim - 1)
    padded = jnp.pad(values, leading + [(NY, NY)])
    column = lax.broadcasted_iota(jnp.int32, (extent,), 0) % NY
    lower_ok = (column != 0).astype(values.dtype)
    upper_ok = (column != NY - 1).astype(values.dtype)
    return (
        padded[..., 0:extent]
        + padded[..., 2 * NY : 2 * NY + extent]
        + padded[..., NY - 1 : NY - 1 + extent] * lower_ok
        + padded[..., NY + 1 : NY + 1 + extent] * upper_ok
    )


def colsum(values):
    return jnp.sum(values, axis=(0, 2))


def on_device(samples, potential):
    nodes = lax.axis_size("shift")
    planes = samples.shape[0]
    order = lax.axis_index("shift").astype(jnp.float32)
    angle = jnp.pi * (order + 0.5) / nodes
    shift_re = CENTRE + RADIUS * jnp.cos(angle)
    shift_im = RADIUS * jnp.sin(angle)
    weight_re = RADIUS * jnp.cos(angle) / nodes
    weight_im = RADIUS * jnp.sin(angle) / nodes

    def inverses(onsite_part):
        diag_re = shift_re - onsite_part
        modulus = diag_re * diag_re + shift_im * shift_im
        return (diag_re / modulus, -shift_im / modulus)

    def apply_inv(vector, inv_pair):
        return jnp.stack(
            [
                vector[0] * inv_pair[0] - vector[1] * inv_pair[1],
                vector[0] * inv_pair[1] + vector[1] * inv_pair[0],
            ]
        )

    def combine(vector, hamil):
        return jnp.stack(
            [
                shift_re * vector[0] - shift_im * vector[1] - hamil[0],
                shift_re * vector[1] + shift_im * vector[0] - hamil[1],
            ]
        )

    onsite = (6.0 + potential)[:, None, :]
    inv_own = inverses(onsite)

    def shrink_operate(vector, onsite_inner):
        inner = vector[:, 1:-1]
        beside = vector[:, 2:] + vector[:, :-2] + plane_sum(inner)
        return combine(inner, onsite_inner * inner - beside)

    joined = jnp.concatenate([samples, potential[:, None, :]], axis=1)
    extended = extended_2(joined, (("dom", 0),), 2)
    ext_samples = extended[:, :-1]
    ext_onsite = 6.0 + extended[:, -1:]
    inv_ext = inverses(ext_onsite)
    first_ext = apply_inv(jnp.stack([ext_samples, jnp.zeros_like(ext_samples)]), inv_ext)
    image_ext = shrink_operate(first_ext, ext_onsite[1:-1])
    total_planes = planes * lax.axis_size("dom")
    plane_index = (
        lax.axis_index("dom") * planes - 1 + lax.broadcasted_iota(jnp.int32, (planes + 2,), 0)
    )
    inside = ((plane_index >= 0) & (plane_index < total_planes)).astype(jnp.float32)
    image_ext = image_ext * inside[None, :, None, None]
    image_one = image_ext[:, 1:-1]
    first_block_real = image_one[0]
    first_block_imag = image_one[1]
    first_set = jnp.stack(
        [
            colsum(first_block_real * first_block_real + first_block_imag * first_block_imag),
            colsum(first_block_real * samples),
            colsum(-first_block_imag * samples),
        ]
    )
    first_tot = lax.psum(first_set, "dom")
    inv_mid = (inv_ext[0][1:-1], inv_ext[1][1:-1])
    image_two = shrink_operate(apply_inv(image_ext, inv_mid), ext_onsite[2:-2])
    two_re = image_two[0]
    two_im = image_two[1]
    second_set = jnp.stack(
        [
            colsum(first_block_real * two_re + first_block_imag * two_im),
            colsum(first_block_real * two_im - first_block_imag * two_re),
            colsum(two_re * two_re + two_im * two_im),
            colsum(two_re * samples),
            colsum(-two_im * samples),
        ]
    )
    second_tot = lax.psum(second_set, "dom")
    totals = jnp.concatenate([first_tot, second_tot], axis=0)
    g_one = totals[0]
    q_one_re = totals[1]
    q_one_im = totals[2]
    g_mix_re = totals[3]
    g_mix_im = totals[4]
    g_two = totals[5]
    q_two_re = totals[6]
    q_two_im = totals[7]
    ridge = RIDGE * (g_one + g_two) / 2.0
    determ = (g_one + ridge) * (g_two + ridge) - (g_mix_re * g_mix_re + g_mix_im * g_mix_im)
    coef_one_re = (
        (g_two + ridge) * q_one_re - (g_mix_re * q_two_re - g_mix_im * q_two_im)
    ) / determ
    coef_one_im = (
        (g_two + ridge) * q_one_im - (g_mix_re * q_two_im + g_mix_im * q_two_re)
    ) / determ
    coef_two_re = (
        (g_one + ridge) * q_two_re - (g_mix_re * q_one_re + g_mix_im * q_one_im)
    ) / determ
    coefficient_second_imag = (
        (g_one + ridge) * q_two_im - (g_mix_re * q_one_im - g_mix_im * q_one_re)
    ) / determ
    first_coefficient_real = coef_one_re[None, :, None]
    first_coefficient_imag = coef_one_im[None, :, None]
    second_coefficient_real = coef_two_re[None, :, None]
    second_coefficient_imag = coefficient_second_imag[None, :, None]
    solution = apply_inv(
        jnp.stack(
            [
                first_coefficient_real * samples
                + second_coefficient_real * first_block_real
                - second_coefficient_imag * first_block_imag,
                first_coefficient_imag * samples
                + second_coefficient_real * first_block_imag
                + second_coefficient_imag * first_block_real,
            ]
        ),
        inv_own,
    )
    weighted = weight_re * solution[0] - weight_im * solution[1]
    scale = 1.0 / (NX * NY * planes * lax.axis_size("dom"))
    subspace = lax.psum(weighted, "shift")
    padded = extended_2(subspace, (("dom", 0),), 1)
    applied = onsite * subspace - (padded[2:] + padded[:-2] + plane_sum(subspace))
    part_h = jnp.einsum("znc,zmc->nm", subspace, applied, precision=lax.Precision.HIGHEST) * scale
    part_b = jnp.einsum("znc,zmc->nm", subspace, subspace, precision=lax.Precision.HIGHEST) * scale
    reduced_h, reduced_b = lax.psum((part_h, part_b), "dom")
    return (subspace, reduced_h, reduced_b)


def solution(mesh):
    in_specs = (P("dom", None, None), P("dom", None))
    out_specs = (P("dom", None, None), P(), P())
    return jax.shard_map(
        on_device, mesh=mesh, in_specs=in_specs, out_specs=out_specs, check_vma=False
    )
```

profile of v0, /device:TPU:0, one launch (start us, length us, event | category | flops | bytes accessed | tf_op | source)
XLA Modules:
  0.0 185.9 jit_solution(1204473247824905076)
XLA Ops:
  7.2 0.0 copy-start.4
  7.2 0.0 all-reduce.7.cloned.1.call-start
  7.2 1.7 constant_dynamic-update-slice_fusion
  9.0 0.0 copy-done.4
  9.0 0.1 dynamic-update-slice.1
  9.1 0.1 fusion.77
  9.2 0.4 copy.8
  9.7 5.0 %collective-permute-start = (f32[2,65,1024]{2,0,1:T(2,128)S(1)}, f32[2,65,1024]{2,0,1:T(2,128)S(1)}, u32[]{:S(2)}, u32[]{:S(2)}) collective-permute-start(f32[2,65,1024]{2,0,1:T(2,128)S(1)} %copy.8), channel_id=1, source_target_pairs={{0,1},{1,2},{2,3},{4,5},{5,6},{6,7},{8,9},{9,10},{10,11},{12,13},{... | collective-permute-start | bytes 1597448 | tf_op jit(solution)/shard_map/ppermute | solution.py:20
  14.7 1.2 copy.9
  15.9 1.3 collective-permute-start.1
  17.3 0.6 broadcast_add_fusion
  18.0 8.0 %collective-permute-done = f32[2,65,1024]{2,0,1:T(2,128)S(1)} collective-permute-done((f32[2,65,1024]{2,0,1:T(2,128)S(1)}, f32[2,65,1024]{2,0,1:T(2,128)S(1)}, u32[]{:S(2)}, u32[]{:S(2)}) %collective-permute-start) | collective-permute-done | bytes 532512 | tf_op jit(solution)/shard_map/ppermute | solution.py:20
  26.0 0.2 copy.10
  26.1 5.5 %collective-permute-done.1 = f32[2,65,1024]{2,0,1:T(2,128)} collective-permute-done((f32[2,65,1024]{2,0,1:T(2,128)}, f32[2,65,1024]{2,0,1:T(2,128)}, u32[]{:S(2)}, u32[]{:S(2)}) %collective-permute-start.1) | collective-permute-done | bytes 532512 | tf_op jit(solution)/shard_map/ppermute | solution.py:21
  31.6 1.2 copy.11
  32.8 0.1 broadcast_subtract_fusion
  32.9 0.1 copy_divide_fusion
  33.0 0.0 copy-start.3
  33.1 0.3 pad_maximum_fusion.2
  33.4 0.2 copy-done.3
  33.7 0.9 add_bitcast_fusion
  34.6 2.8 %fusion.9 = f32[2,10,64,1024]{3,2,1,0:T(8,128)} fusion(f32[1,12,64,1024]{3,2,1,0:T(8,128)S(1)} %get-tuple-element.29, f32[1,12,64,1024]{3,2,1,0:T(8,128)S(1)} %get-tuple-element.28), kind=kLoop, calls=%fused_computation.21 | loop fusion | flops 1310720 | bytes 11534336 | tf_op jit(solution)/shard_map/stack | solution.py:61
  37.4 13.4 %fusion.4 = f32[2,10,64,1024]{3,2,1,0:T(8,128)} fusion(f32[2,10,64,1024]{3,2,1,0:T(8,128)} %fusion.9, f32[1,12,64,1024]{3,2,1,0:T(8,128)S(1)} %get-tuple-element.29, f32[1,12,64,1024]{3,2,1,0:T(8,128)S(1)} %get-tuple-element.28, f32[1024]{0:T(1024)S(1)} %get-tuple-element.45, f32[1024]{0:T(1024)S(1)} %get-tuple-element.44, f32[10,1024]{1,0:T(8,128)S(1)} %bitcast.188), kind=kLoop, calls=%fused_computation.16 | loop fusion | flops 14417920 | bytes 16826368 | tf_op jit(solution)/shard_map/sub | solution.py:82
  50.8 3.8 %slice_subtract_fusion.1 = (f32[1,10,64,1024]{3,2,1,0:T(8,128)S(1)}, f32[1,10,64,1024]{3,2,1,0:T(8,128)S(1)}) fusion(f32[2,10,64,1024]{3,2,1,0:T(8,128)} %fusion.4, f32[1,12,64,1024]{3,2,1,0:T(8,128)S(1)} %get-tuple-element.28, f32[1,12,64,1024]{3,2,1,0:T(8,128)S(1)} %get-tuple-element.29, f32[]{:T(128)S(6)} %mul.491, f32[]{:T(128)S(6)} %add_shard_map.3), kind=kLoop, calls=%fused_computation.43 | loop fusion | flops 5242880 | bytes 15728648 | tf_op jit(solution)/shard_map/sub | solution.py:71
  54.6 0.0 slice-done
  54.7 0.9 maximum_multiply_fusion
  55.6 1.3 multiply_add_fusion
  56.8 0.6 fusion.19
  57.4 4.8 %fusion.14 = f32[2,8,64,1024]{3,2,1,0:T(8,128)S(1)} fusion(f32[2,8,64,1024]{3,2,1,0:T(8,128)S(1)} %fusion.19, f32[1,10,64,1024]{3,2,1,0:T(8,128)S(1)} %get-tuple-element.27, f32[1,10,64,1024]{3,2,1,0:T(8,128)S(1)} %get-tuple-element.26, f32[1024]{0:T(1024)S(1)} %get-tuple-element.45, f32[1024]{0:T(1024)S(1)} %get-tuple-element.44, f32[8,1024]{1,0:T(8,128)S(1)} %bitcast.189), kind=kLoop, calls=%fused_computation.32 | loop fusion | flops 11534336 | bytes 13672448 | tf_op jit(solution)/shard_map/sub | solution.py:82
  62.3 0.0 copy-start.2
  62.3 1.5 fusion.36
  63.8 0.1 copy-done.2
  63.9 2.0 %multiply_reduce_fusion.1 = (f32[64]{0:T(128)S(1)}, f32[64]{0:T(128)S(1)}, f32[64]{0:T(128)S(1)}, f32[64]{0:T(128)S(1)}, f32[64]{0:T(128)S(1)}, /*index=5*/f32[64]{0:T(128)S(1)}, f32[64]{0:T(128)S(1)}, f32[64]{0:T(128)S(1)}) fusion(f32[8,64,1024]{2,1,0:T(8,128)S(1)} %copy-done.2, f32[2,10,64,1024]{3,2,1,0:T(8,128)S(1)} %maximum_multiply_fusion, ...), kind=kLoop, calls=%fused_computation.72 | loop fusion | flops 13630976 | bytes 10487808 | tf_op jit(solution)/shard_map/reduce_sum | solution.py:42
  66.0 10.3 %all-reduce.4 = (f32[5,64]{1,0:T(8,128)S(1)}, f32[3,64]{1,0:T(4,128)S(1)}) all-reduce(f32[5,64]{1,0:T(8,128)S(1)} %stack.59, f32[3,64]{1,0:T(4,128)S(1)} %pad_maximum_fusion.6), channel_id=1, replica_groups=mesh['shift'=8,'dom'=4] {'dom'}, use_global_device_ids=true, to_apply=%region_5.6 | all-reduce | flops 512 | bytes 4096 | tf_op jit(solution)/shard_map/psum | solution.py:121
  76.3 4.9 %multiply_subtract_fusion.1 = f32[8,64,1024]{2,1,0:T(8,128)} fusion(f32[8,64,1024]{2,1,0:T(8,128)S(1)} %copy-done.2, f32[2,10,64,1024]{3,2,1,0:T(8,128)} %copy-done, f32[]{:T(128)S(6)} %div.77, f32[8,1024]{1,0:T(8,128)S(1)} %get-tuple-element.38, f32[64]{0:T(128)S(1)} %fusion.65, f32[8,1024]{1,0:T(8,128)S(1)} %get-tuple-element.39, ...), kind=kLoop, calls=%fused_computation.70 | loop fusion | flops 9961472 | bytes 8455176 | tf_op jit(solution)/shard_map/sub | solution.py:162
  81.2 0.0 all-reduce.7.cloned.1.call-update
  81.2 0.0 copy-start.5
  81.3 60.2 %all-reduce.7.cloned.1.call-done = f32[8,64,1024]{2,1,0:T(8,128)} async-done(((f32[8,64,1024]{2,1,0:T(8,128)}), f32[8,64,1024]{2,1,0:T(8,128)}) %all-reduce.7.cloned.1.call-update) | async-done | bytes 2097168 | tf_op jit(solution)/shard_map/psum | solution.py:164
  141.5 1.2 fusion.78
  142.7 1.3 collective-permute-start.2
  144.0 4.6 %collective-permute-start.3 = (f32[1,64,1024]{2,1,0:T(8,128)S(1)}, f32[1,64,1024]{2,1,0:T(8,128)S(1)}, u32[]{:S(2)}, u32[]{:S(2)}) collective-permute-start(f32[1,64,1024]{2,1,0:T(8,128)S(1)} %get-tuple-element.33), channel_id=1, source_target_pairs={{0,1},{1,2},{2,3},{4,5},{5,6},{6,7},{8,9},{9,10},{10,11},{12,13},{... | collective-permute-start | bytes 786440 | tf_op jit(solution)/shard_map/ppermute | solution.py:20
  148.6 4.0 %fusion.41 = f32[64,64]{1,0:T(8,128)S(1)} fusion(f32[8,64,1024]{2,1,0:T(8,128)} %all-reduce.7.cloned.1.call-done), kind=kOutput, calls=%fused_computation.81 | convolution fusion | flops 402657280 | bytes 2113536 | tf_op jit(solution)/shard_map/znc,zmc->nm/dot_general | solution.py:168
  152.6 0.0 collective-permute-done.2
  152.6 0.0 collective-permute-done.3
  152.7 0.0 copy-done.1
  152.7 3.8 %fusion.42 = f32[64,64]{1,0:T(8,128)S(1)} fusion(f32[8,64,1024]{2,1,0:T(8,128)S(1)} %copy-done.1, f32[1,64,1024]{2,1,0:T(8,128)S(1)} %collective-permute-done.3, f32[1,64,1024]{2,1,0:T(8,128)S(1)} %collective-permute-done.2, f32[1024]{0:T(1024)S(1)} %get-tuple-element.45, f32[1024]{0:T(1024)S(1)} %get-tuple-element.44, f32[8,1024]{1,0:T(8,128)S(1)} %copy-done.5), kind=kOutput, calls=%fused_computation.82 | convolution fusion | flops 408424448 | bytes 4775936 | tf_op jit(solution)/shard_map/znc,zmc->nm/dot_general | solution.py:167
  156.5 21.2 %all-reduce.3 = (f32[64,64]{1,0:T(8,128)}, f32[64,64]{1,0:T(8,128)}) all-reduce(f32[64,64]{1,0:T(8,128)S(1)} %fusion.42, f32[64,64]{1,0:T(8,128)S(1)} %fusion.41), channel_id=1, replica_groups=mesh['shift'=8,'dom'=4] {'dom'}, use_global_device_ids=true, to_apply=%region_11.12 | all-reduce | flops 8192 | bytes 65536 | tf_op jit(solution)/shard_map/psum | solution.py:169
  177.7 1.3 copy.40
  (21 shorter events, 0.2 us)
Async XLA Ops:
  7.2 1.8 copy-start.4
  7.2 134.3 %all-reduce.7.cloned.1.call-start = ((), (), s32[]{:S(2)}) async-start(), calls=%async_computation | async-start | bytes 4194304 | tf_op jit(solution)/shard_map/psum | solution.py:164
  9.7 16.3 %collective-permute-start = (f32[2,65,1024]{2,0,1:T(2,128)S(1)}, f32[2,65,1024]{2,0,1:T(2,128)S(1)}, u32[]{:S(2)}, u32[]{:S(2)}) collective-permute-start(f32[2,65,1024]{2,0,1:T(2,128)S(1)} %copy.8), channel_id=1, source_target_pairs={{0,1},{1,2},{2,3},{4,5},{5,6},{6,7},{8,9},{9,10},{10,11},{12,13},{... | collective-permute-start | bytes 1597448 | tf_op jit(solution)/shard_map/ppermute | solution.py:20
  15.9 15.8 %collective-permute-start.1 = (f32[2,65,1024]{2,0,1:T(2,128)}, f32[2,65,1024]{2,0,1:T(2,128)}, u32[]{:S(2)}, u32[]{:S(2)}) collective-permute-start(f32[2,65,1024]{2,0,1:T(2,128)} %copy.9), channel_id=1, source_target_pairs={{1,0},{2,1},{3,2},{5,4},{6,5},{7,6},{9,8},{10,9},{11,10},{13,12},{... | collective-permute-start | bytes 1597448 | tf_op jit(solution)/shard_map/ppermute | solution.py:21
  33.0 0.7 copy-start.3
  50.8 3.9 %slice-start = ((f32[12,1,1024]{2,1,0:T(1,128)}), f32[10,1,1024]{2,1,0:T(1,128)S(1)}, s32[]{:S(2)}) async-start(f32[12,1,1024]{2,1,0:T(1,128)} %copy-done.3), calls=%async_computation.1 | async-start | bytes 81920 | tf_op jit(solution)/shard_map/slice | solution.py:108
  55.6 8.2 %copy-start = (f32[2,10,64,1024]{3,2,1,0:T(8,128)}, f32[2,10,64,1024]{3,2,1,0:T(8,128)S(1)}, u32[]{:S(2)}) copy-start(f32[2,10,64,1024]{3,2,1,0:T(8,128)S(1)} %maximum_multiply_fusion) | copy-start | bytes 15728644
  62.3 1.6 copy-start.2
  81.2 71.4 %copy-start.5 = (f32[8,1024]{1,0:T(8,128)S(1)}, f32[8,1024]{1,0:T(8,128)}, u32[]{:S(2)}) copy-start(f32[8,1024]{1,0:T(8,128)} %get-tuple-element.37) | copy-start | bytes 98308
  141.5 11.2 %copy-start.1 = (f32[8,64,1024]{2,1,0:T(8,128)S(1)}, f32[8,64,1024]{2,1,0:T(8,128)}, u32[]{:S(2)}) copy-start(f32[8,64,1024]{2,1,0:T(8,128)} %all-reduce.7.cloned.1.call-done) | copy-start | bytes 6291460
  142.7 9.9 %collective-permute-start.2 = (f32[1,64,1024]{2,1,0:T(8,128)S(1)}, f32[1,64,1024]{2,1,0:T(8,128)S(1)}, u32[]{:S(2)}, u32[]{:S(2)}) collective-permute-start(f32[1,64,1024]{2,1,0:T(8,128)S(1)} %get-tuple-element.32), channel_id=1, source_target_pairs={{1,0},{2,1},{3,2},{5,4},{6,5},{7,6},{9,8},{10,9},{11,10},{13,12},{... | collective-permute-start | bytes 786440 | tf_op jit(solution)/shard_map/ppermute | solution.py:21
  144.0 8.7 %collective-permute-start.3 = (f32[1,64,1024]{2,1,0:T(8,128)S(1)}, f32[1,64,1024]{2,1,0:T(8,128)S(1)}, u32[]{:S(2)}, u32[]{:S(2)}) collective-permute-start(f32[1,64,1024]{2,1,0:T(8,128)S(1)} %get-tuple-element.33), channel_id=1, source_target_pairs={{0,1},{1,2},{2,3},{4,5},{5,6},{6,7},{8,9},{9,10},{10,11},{12,13},{... | collective-permute-start | bytes 786440 | tf_op jit(solution)/shard_map/ppermute | solution.py:20
Sparse Core Ops, SparseCore 0:
  81.4 60.0 all-reduce.6
where the time goes:
time: 186 us
  waiting for transfers between devices  73.8 us (40%)
  other arithmetic  38.1 us (20%)
  blocking collectives  31.5 us (17%)
  between operations  14.5 us (8%)
  starting transfers between devices  12.2 us (7%)
  local copies, waits for them, and re-layouts  7.97 us (4%)
  matrix products  7.85 us (4%)
    psum x1, waiting for transfers between devices, on_device(): subspace = lax.psum(weighted, 'shift')  60.2 us
    psum x1, blocking collectives, on_device(): reduced_h, reduced_b = lax.psum((part_h, part_b), 'dom')  21.2 us
    sub x2, other arithmetic, shrink_operate(): return combine(inner, onsite_inner * inner - beside)  18.2 us
    psum x1, blocking collectives, on_device(): second_tot = lax.psum(second_set, 'dom')  10.3 us
    ppermute x2, starting transfers between devices, extended_2(): before = lax.ppermute(last, axis, up)  9.55 us
    ppermute x2, waiting for transfers between devices, extended_2(): before = lax.ppermute(last, axis, up)  8.03 us
    ppermute x2, waiting for transfers between devices, extended_2(): after = lax.ppermute(first, axis, down)  5.49 us
    sub x2, other arithmetic, combine(): shift_re * vector[0] - shift_im * vector[1] - hamil[0]  5.3 us
  transfers between devices with their start and end apart: 5, of which 3 were waited for; matrix products, arithmetic and copies ran while one was open for 3% of the time, Pallas kernels for 0%

commit v1 on v0

--- a/solution.py
+++ b/solution.py
@@ -118,7 +118,7 @@
             colsum(-two_im * samples),
         ]
     )
-    second_tot = lax.psum(second_set, "dom")
+    second_tot = jnp.sum(lax.all_gather(second_set, "dom"), axis=0)
     totals = jnp.concatenate([first_tot, second_tot], axis=0)
     g_one = totals[0]
     q_one_re = totals[1]

time: 186 us -> 199 us (1.070)
  blocking collectives: 31.5 us -> 44.6 us
    all_gather x0 -> x1, blocking collectives: none -> 13.4 us  [on_device(): second_tot = jnp.sum(lax.all_gather(second_set, 'dom'), axis=0)]
where the time goes in v1:
time: 199 us
  waiting for transfers between devices  73.7 us (37%)
  blocking collectives  44.6 us (22%)
  other arithmetic  38.1 us (19%)
  between operations  14.5 us (7%)
  starting transfers between devices  12.2 us (6%)
  local copies, waits for them, and re-layouts  7.97 us (4%)
  matrix products  7.85 us (4%)
    psum x1, waiting for transfers between devices, on_device(): subspace = lax.psum(weighted, 'shift')  60.2 us
    psum x1, blocking collectives, on_device(): reduced_h, reduced_b = lax.psum((part_h, part_b), 'dom')  21.2 us
    sub x2, other arithmetic, shrink_operate(): return combine(inner, onsite_inner * inner - beside)  18.2 us
    all_gather x1, blocking collectives, on_device(): second_tot = jnp.sum(lax.all_gather(second_set, 'dom'), axis=0)  13.4 us
    psum x1, blocking collectives, on_device(): first_tot = lax.psum(first_set, 'dom')  9.92 us
    ppermute x2, starting transfers between devices, extended_2(): before = lax.ppermute(last, axis, up)  9.55 us
    ppermute x2, waiting for transfers between devices, extended_2(): before = lax.ppermute(last, axis, up)  8.03 us
    ppermute x2, waiting for transfers between devices, extended_2(): after = lax.ppermute(first, axis, down)  5.49 us
  transfers between devices with their start and end apart: 5, of which 3 were waited for; matrix products, arithmetic and copies ran while one was open for 3% of the time, Pallas kernels for 0%

profile of v1, /device:TPU:0, one launch (start us, length us, event | category | flops | bytes accessed | tf_op | source)
XLA Modules:
  0.0 198.9 jit_solution(7608729000263703940)
XLA Ops:
  7.2 0.0 copy-start.4
  7.2 0.0 all-reduce.6.cloned.1.call-start
  7.2 1.7 constant_dynamic-update-slice_fusion
  9.0 0.0 copy-done.4
  9.0 0.1 dynamic-update-slice.1
  9.1 0.1 fusion.77
  9.2 0.4 copy.8
  9.7 5.0 %collective-permute-start = (f32[2,65,1024]{2,0,1:T(2,128)S(1)}, f32[2,65,1024]{2,0,1:T(2,128)S(1)}, u32[]{:S(2)}, u32[]{:S(2)}) collective-permute-start(f32[2,65,1024]{2,0,1:T(2,128)S(1)} %copy.8), channel_id=1, source_target_pairs={{0,1},{1,2},{2,3},{4,5},{5,6},{6,7},{8,9},{9,10},{10,11},{12,13},{... | collective-permute-start | bytes 1597448 | tf_op jit(solution)/shard_map/ppermute | solution.py:20
  14.7 1.2 copy.9
  15.9 1.3 collective-permute-start.1
  17.3 0.6 broadcast_add_fusion
  18.0 8.0 %collective-permute-done = f32[2,65,1024]{2,0,1:T(2,128)S(1)} collective-permute-done((f32[2,65,1024]{2,0,1:T(2,128)S(1)}, f32[2,65,1024]{2,0,1:T(2,128)S(1)}, u32[]{:S(2)}, u32[]{:S(2)}) %collective-permute-start) | collective-permute-done | bytes 532512 | tf_op jit(solution)/shard_map/ppermute | solution.py:20
  26.0 0.2 copy.10
  26.1 5.5 %collective-permute-done.1 = f32[2,65,1024]{2,0,1:T(2,128)} collective-permute-done((f32[2,65,1024]{2,0,1:T(2,128)}, f32[2,65,1024]{2,0,1:T(2,128)}, u32[]{:S(2)}, u32[]{:S(2)}) %collective-permute-start.1) | collective-permute-done | bytes 532512 | tf_op jit(solution)/shard_map/ppermute | solution.py:21
  31.6 1.2 copy.11
  32.8 0.1 broadcast_subtract_fusion
  32.9 0.1 copy_divide_fusion
  33.0 0.0 copy-start.3
  33.1 0.3 pad_maximum_fusion.2
  33.4 0.2 copy-done.3
  33.7 0.9 add_bitcast_fusion
  34.6 2.8 %fusion.9 = f32[2,10,64,1024]{3,2,1,0:T(8,128)} fusion(f32[1,12,64,1024]{3,2,1,0:T(8,128)S(1)} %get-tuple-element.27, f32[1,12,64,1024]{3,2,1,0:T(8,128)S(1)} %get-tuple-element.26), kind=kLoop, calls=%fused_computation.21 | loop fusion | flops 1310720 | bytes 11534336 | tf_op jit(solution)/shard_map/stack | solution.py:61
  37.4 13.4 %fusion.4 = f32[2,10,64,1024]{3,2,1,0:T(8,128)} fusion(f32[2,10,64,1024]{3,2,1,0:T(8,128)} %fusion.9, f32[1,12,64,1024]{3,2,1,0:T(8,128)S(1)} %get-tuple-element.27, f32[1,12,64,1024]{3,2,1,0:T(8,128)S(1)} %get-tuple-element.26, f32[1024]{0:T(1024)S(1)} %get-tuple-element.43, f32[1024]{0:T(1024)S(1)} %get-tuple-element.42, f32[10,1024]{1,0:T(8,128)S(1)} %bitcast.189), kind=kLoop, calls=%fused_computation.16 | loop fusion | flops 14417920 | bytes 16826368 | tf_op jit(solution)/shard_map/sub | solution.py:82
  50.8 3.8 %slice_subtract_fusion.1 = (f32[1,10,64,1024]{3,2,1,0:T(8,128)S(1)}, f32[1,10,64,1024]{3,2,1,0:T(8,128)S(1)}) fusion(f32[2,10,64,1024]{3,2,1,0:T(8,128)} %fusion.4, f32[1,12,64,1024]{3,2,1,0:T(8,128)S(1)} %get-tuple-element.26, f32[1,12,64,1024]{3,2,1,0:T(8,128)S(1)} %get-tuple-element.27, f32[]{:T(128)S(6)} %mul.491, f32[]{:T(128)S(6)} %add_shard_map.3), kind=kLoop, calls=%fused_computation.43 | loop fusion | flops 5242880 | bytes 15728648 | tf_op jit(solution)/shard_map/sub | solution.py:71
  54.6 0.0 slice-done
  54.7 0.9 maximum_multiply_fusion
  55.6 1.3 multiply_add_fusion
  56.8 0.6 fusion.19
  57.4 4.8 %fusion.14 = f32[2,8,64,1024]{3,2,1,0:T(8,128)S(1)} fusion(f32[2,8,64,1024]{3,2,1,0:T(8,128)S(1)} %fusion.19, f32[1,10,64,1024]{3,2,1,0:T(8,128)S(1)} %get-tuple-element.25, f32[1,10,64,1024]{3,2,1,0:T(8,128)S(1)} %get-tuple-element.24, f32[1024]{0:T(1024)S(1)} %get-tuple-element.43, f32[1024]{0:T(1024)S(1)} %get-tuple-element.42, f32[8,1024]{1,0:T(8,128)S(1)} %bitcast.190), kind=kLoop, calls=%fused_computation.32 | loop fusion | flops 11534336 | bytes 13672448 | tf_op jit(solution)/shard_map/sub | solution.py:82
  62.3 0.0 copy-start.2
  62.3 1.5 fusion.36
  63.8 0.1 copy-done.2
  63.9 2.0 %multiply_reduce_fusion.1 = (f32[64]{0:T(128)S(1)}, f32[64]{0:T(128)S(1)}, f32[64]{0:T(128)S(1)}, f32[64]{0:T(128)S(1)}, f32[64]{0:T(128)S(1)}, /*index=5*/f32[64]{0:T(128)S(1)}, f32[64]{0:T(128)S(1)}, f32[64]{0:T(128)S(1)}) fusion(f32[8,64,1024]{2,1,0:T(8,128)S(1)} %copy-done.2, f32[2,10,64,1024]{3,2,1,0:T(8,128)S(1)} %maximum_multiply_fusion, ...), kind=kLoop, calls=%fused_computation.72 | loop fusion | flops 13630976 | bytes 10487808 | tf_op jit(solution)/shard_map/reduce_sum | solution.py:42
  65.9 9.9 %psum.28 = f32[3,64]{1,0:T(4,128)S(1)} all-reduce(f32[3,64]{1,0:T(4,128)S(1)} %pad_maximum_fusion.6), channel_id=1, replica_groups=mesh['shift'=8,'dom'=4] {'dom'}, use_global_device_ids=true, to_apply=%region_9.10 | all-reduce | flops 192 | bytes 1536 | tf_op jit(solution)/shard_map/psum | solution.py:107
  75.9 13.4 %all-gather.1 = f32[4,5,64]{2,1,0:T(8,128)S(1)} all-gather(f32[1,5,64]{2,1,0:T(8,128)S(1)} %bitcast.191), channel_id=2, replica_groups=mesh['shift'=8,'dom'=4] {'dom'}, dimensions={0}, use_global_device_ids=true | all-gather | bytes 6400 | tf_op jit(solution)/shard_map/all_gather | solution.py:121
  89.4 4.9 %multiply_subtract_fusion.1 = f32[8,64,1024]{2,1,0:T(8,128)} fusion(f32[8,64,1024]{2,1,0:T(8,128)S(1)} %copy-done.2, f32[2,10,64,1024]{3,2,1,0:T(8,128)} %copy-done, f32[]{:T(128)S(6)} %div.77, f32[8,1024]{1,0:T(8,128)S(1)} %get-tuple-element.36, f32[64]{0:T(128)S(1)} %fusion.65, f32[8,1024]{1,0:T(8,128)S(1)} %get-tuple-element.37, ...), kind=kLoop, calls=%fused_computation.70 | loop fusion | flops 9961472 | bytes 8455176 | tf_op jit(solution)/shard_map/sub | solution.py:162
  94.3 0.0 all-reduce.6.cloned.1.call-update
  94.3 0.0 copy-start.5
  94.3 60.2 %all-reduce.6.cloned.1.call-done = f32[8,64,1024]{2,1,0:T(8,128)} async-done(((f32[8,64,1024]{2,1,0:T(8,128)}), f32[8,64,1024]{2,1,0:T(8,128)}) %all-reduce.6.cloned.1.call-update) | async-done | bytes 2097168 | tf_op jit(solution)/shard_map/psum | solution.py:164
  154.5 1.2 fusion.78
  155.8 1.3 collective-permute-start.2
  157.1 4.6 %collective-permute-start.3 = (f32[1,64,1024]{2,1,0:T(8,128)S(1)}, f32[1,64,1024]{2,1,0:T(8,128)S(1)}, u32[]{:S(2)}, u32[]{:S(2)}) collective-permute-start(f32[1,64,1024]{2,1,0:T(8,128)S(1)} %get-tuple-element.31), channel_id=1, source_target_pairs={{0,1},{1,2},{2,3},{4,5},{5,6},{6,7},{8,9},{9,10},{10,11},{12,13},{... | collective-permute-start | bytes 786440 | tf_op jit(solution)/shard_map/ppermute | solution.py:20
  161.6 4.0 %fusion.41 = f32[64,64]{1,0:T(8,128)S(1)} fusion(f32[8,64,1024]{2,1,0:T(8,128)} %all-reduce.6.cloned.1.call-done), kind=kOutput, calls=%fused_computation.81 | convolution fusion | flops 402657280 | bytes 2113536 | tf_op jit(solution)/shard_map/znc,zmc->nm/dot_general | solution.py:168
  165.7 0.0 collective-permute-done.2
  165.7 0.0 collective-permute-done.3
  165.7 3.8 %fusion.42 = f32[64,64]{1,0:T(8,128)S(1)} fusion(f32[8,64,1024]{2,1,0:T(8,128)S(1)} %copy-done.1, f32[1,64,1024]{2,1,0:T(8,128)S(1)} %collective-permute-done.3, f32[1,64,1024]{2,1,0:T(8,128)S(1)} %collective-permute-done.2, f32[1024]{0:T(1024)S(1)} %get-tuple-element.43, f32[1024]{0:T(1024)S(1)} %get-tuple-element.42, f32[8,1024]{1,0:T(8,128)S(1)} %copy-done.5), kind=kOutput, calls=%fused_computation.82 | convolution fusion | flops 408424448 | bytes 4775936 | tf_op jit(solution)/shard_map/znc,zmc->nm/dot_general | solution.py:167
  169.5 21.2 %all-reduce.3 = (f32[64,64]{1,0:T(8,128)}, f32[64,64]{1,0:T(8,128)}) all-reduce(f32[64,64]{1,0:T(8,128)S(1)} %fusion.42, f32[64,64]{1,0:T(8,128)S(1)} %fusion.41), channel_id=1, replica_groups=mesh['shift'=8,'dom'=4] {'dom'}, use_global_device_ids=true, to_apply=%region_11.12 | all-reduce | flops 8192 | bytes 65536 | tf_op jit(solution)/shard_map/psum | solution.py:169
  190.8 1.3 copy.40
  (23 shorter events, 0.2 us)
Async XLA Ops:
  7.2 1.8 copy-start.4
  7.2 147.4 %all-reduce.6.cloned.1.call-start = ((), (), s32[]{:S(2)}) async-start(), calls=%async_computation | async-start | bytes 4194304 | tf_op jit(solution)/shard_map/psum | solution.py:164
  9.7 16.3 %collective-permute-start = (f32[2,65,1024]{2,0,1:T(2,128)S(1)}, f32[2,65,1024]{2,0,1:T(2,128)S(1)}, u32[]{:S(2)}, u32[]{:S(2)}) collective-permute-start(f32[2,65,1024]{2,0,1:T(2,128)S(1)} %copy.8), channel_id=1, source_target_pairs={{0,1},{1,2},{2,3},{4,5},{5,6},{6,7},{8,9},{9,10},{10,11},{12,13},{... | collective-permute-start | bytes 1597448 | tf_op jit(solution)/shard_map/ppermute | solution.py:20
  15.9 15.8 %collective-permute-start.1 = (f32[2,65,1024]{2,0,1:T(2,128)}, f32[2,65,1024]{2,0,1:T(2,128)}, u32[]{:S(2)}, u32[]{:S(2)}) collective-permute-start(f32[2,65,1024]{2,0,1:T(2,128)} %copy.9), channel_id=1, source_target_pairs={{1,0},{2,1},{3,2},{5,4},{6,5},{7,6},{9,8},{10,9},{11,10},{13,12},{... | collective-permute-start | bytes 1597448 | tf_op jit(solution)/shard_map/ppermute | solution.py:21
  33.0 0.7 copy-start.3
  50.8 3.9 %slice-start = ((f32[12,1,1024]{2,1,0:T(1,128)}), f32[10,1,1024]{2,1,0:T(1,128)S(1)}, s32[]{:S(2)}) async-start(f32[12,1,1024]{2,1,0:T(1,128)} %copy-done.3), calls=%async_computation.1 | async-start | bytes 81920 | tf_op jit(solution)/shard_map/slice | solution.py:108
  55.6 8.2 %copy-start = (f32[2,10,64,1024]{3,2,1,0:T(8,128)}, f32[2,10,64,1024]{3,2,1,0:T(8,128)S(1)}, u32[]{:S(2)}) copy-start(f32[2,10,64,1024]{3,2,1,0:T(8,128)S(1)} %maximum_multiply_fusion) | copy-start | bytes 15728644
  62.3 1.6 copy-start.2
  94.3 71.4 %copy-start.5 = (f32[8,1024]{1,0:T(8,128)S(1)}, f32[8,1024]{1,0:T(8,128)}, u32[]{:S(2)}) copy-start(f32[8,1024]{1,0:T(8,128)} %get-tuple-element.35) | copy-start | bytes 98308
  154.5 11.2 %copy-start.1 = (f32[8,64,1024]{2,1,0:T(8,128)S(1)}, f32[8,64,1024]{2,1,0:T(8,128)}, u32[]{:S(2)}) copy-start(f32[8,64,1024]{2,1,0:T(8,128)} %all-reduce.6.cloned.1.call-done) | copy-start | bytes 6291460
  155.8 9.9 %collective-permute-start.2 = (f32[1,64,1024]{2,1,0:T(8,128)S(1)}, f32[1,64,1024]{2,1,0:T(8,128)S(1)}, u32[]{:S(2)}, u32[]{:S(2)}) collective-permute-start(f32[1,64,1024]{2,1,0:T(8,128)S(1)} %get-tuple-element.30), channel_id=1, source_target_pairs={{1,0},{2,1},{3,2},{5,4},{6,5},{7,6},{9,8},{10,9},{11,10},{13,12},{... | collective-permute-start | bytes 786440 | tf_op jit(solution)/shard_map/ppermute | solution.py:21
  157.1 8.7 %collective-permute-start.3 = (f32[1,64,1024]{2,1,0:T(8,128)S(1)}, f32[1,64,1024]{2,1,0:T(8,128)S(1)}, u32[]{:S(2)}, u32[]{:S(2)}) collective-permute-start(f32[1,64,1024]{2,1,0:T(8,128)S(1)} %get-tuple-element.31), channel_id=1, source_target_pairs={{0,1},{1,2},{2,3},{4,5},{5,6},{6,7},{8,9},{9,10},{10,11},{12,13},{... | collective-permute-start | bytes 786440 | tf_op jit(solution)/shard_map/ppermute | solution.py:20
Sparse Core Ops, SparseCore 0:
  94.4 60.0 all-reduce.5
